TPU v7x, 256 devices: a whole 4x4x8 slice. The times are simulated.
256 devices in a mesh: grp: 8 (over x, core), mem: 32 (over z, y).
Axes of the slice: x: 4, y: 4, z: 8, core: 2. Of those that a mesh axis runs over, the one named last changes fastest.
Arguments:
- slab: float32 [2048, 16384], P('mem', 'grp'), may hold values from 0 to 32, as said below
- tiles: float32 [8192, 16384], P('grp', 'mem'), may hold values from 0 to 1.05, as said below
- slot_rows: int32 [16, 32], P('grp'), may hold values from -1 to 3, as said below
Outputs:
- clustered: float32 [2048, 16384], P('grp', 'mem')
Inputs may be any that keep to these rules, and one draw needn't show every extreme that they name: For each group g and block column m, the used slots h (slot_rows[g * 2 + h, m] >= 0) come first and name distinct block rows of the group; unused slots hold -1. Each block column has at least one used slot in every group, and in every draw some group and block column has all 2 slots used. Entries are nonnegative, positive in the tiles of used slots, and zero in the tiles of unused slots. `slab`: entries are positive.
All inputs are finite; a program needn't handle non-finite values.
Results may differ from a plain program's by a relative error of at most 0.0003.
Values sent between devices are 32-bit elements; how exact they have to be, the bound alone decides.
A program may use at most 64 MiB of HBM per device.

v0:
```python
import jax
import jax.numpy as jnp
from jax import lax
from jax.sharding import PartitionSpec as P


def per_device(slab, tiles, slot_rows):
    tile_size = tiles.shape[1]
    slot_total = tiles.shape[0] // tile_size
    member = lax.axis_index("mem")
    own_rows = lax.dynamic_index_in_dim(slot_rows, member, axis=1, keepdims=False)
    used_slots = jnp.sum((own_rows >= 0).astype(jnp.int32))
    block_rows = jnp.maximum(own_rows, 0)
    tile_stack = tiles.reshape(slot_total, tile_size, tile_size)
    row_piece = lax.all_gather(slab, "mem", axis=0, tiled=True)

    def add_slot(slot_index, running):
        columns = lax.dynamic_slice_in_dim(
            row_piece, block_rows[slot_index] * tile_size, tile_size, 1
        )
        return running + jnp.dot(
            columns,
            tile_stack[slot_index],
            preferred_element_type=jnp.float32,
            precision=lax.Precision.HIGHEST,
        )

    partial_sums = lax.fori_loop(
        0, used_slots, add_slot, jnp.zeros((row_piece.shape[0], tile_size), jnp.float32)
    )
    window_rows = partial_sums.shape[0]
    expanded = lax.psum_scatter(partial_sums, "grp", scatter_dimension=0, tiled=True)
    inflated = expanded * expanded
    column_sums = lax.psum(jnp.sum(inflated, axis=0), "grp")
    column_means = column_sums / window_rows
    return inflated / column_means


def solution(mesh):
    return jax.shard_map(
        per_device,
        mesh=mesh,
        in_specs=(P("mem", "grp"), P("grp", "mem"), P("grp", None)),
        out_specs=P("grp", "mem"),
        check_vma=False,
    )
```

profile of v0, /device:TPU:1, one launch (start us, length us, event | category | flops | bytes accessed | tf_op | source)
XLA Modules:
  0.0 241.1 jit_solution(9636385513887879012)
XLA Ops:
  6.5 0.0 copy-start
  6.5 0.0 all-gather.2.cloned.1.call-start
  6.5 0.7 all-gather.2.cloned.1.call-update
  7.3 0.0 reduce-scatter.2.cloned.1.call-start
  7.3 1.4 maximum_reduce_fusion
  8.8 143.9 %all-gather.2.cloned.1.call-done = f32[2048,2048]{1,0:T(8,128)} async-done(((f32[64,2048]{1,0:T(8,128)}), f32[2048,2048]{1,0:T(8,128)}) %all-gather.2.cloned.1.call-update) | async-done | bytes 16777232 | tf_op jit(solution)/shard_map/all_gather | solution.py:15
  152.7 2.5 %broadcast_in_dim.4 = f32[2048,512]{1,0:T(8,128)} broadcast(f32[]{:T(128)} %constant.7.clone.1), dimensions={} | broadcast | bytes 4194308 | tf_op jit(solution)/shard_map/broadcast_in_dim | solution.py:29
  155.2 0.0 copy-done
  155.2 25.2 %while.10 = (s32[]{:T(128)}, f32[2048,512]{1,0:T(8,128)}, s32[]{:T(128)}, s32[2]{0:T(128)S(1)}, f32[2048,2048]{1,0:T(8,128)}, /*index=5*/f32[2,512,512]{2,1,0:T(...) while((s32[]{:T(128)}, f32[2048,512]{1,0:T(8,128)}, s32[]{:T(128)}, ...), condition=%wide.region_2.3_spmd, body=%wide.region_1.2_spmd.sunk | while | flops 6443499520 | bytes 13631705 | solution.py:28
  155.8 0.6 dynamic_slice.29
  157.0 10.4 %fusion.14 = f32[2048,512]{1,0:T(8,128)} fusion(f32[2048,512]{1,0:T(8,128)} %get-tuple-element.103, f32[2048,2048]{1,0:T(8,128)} %get-tuple-element.117, s32[]{:T(128)S(6)} %select_n.15, f32[2,512,512]{2,1,0:T(8,128)S(1)} %get-tuple-element.118, s32[]{:T(128)S(6)} %select_n.14), kind=kOutput, calls=%fused_computation.2.clone.1 | convolution fusion | flops 6443499520 | bytes 13631496 | tf_op jit(solution)/shard_map/while/body/dot_general | solution.py:21
  168.1 0.6 dynamic_slice.29
  169.3 10.4 %fusion.14 = f32[2048,512]{1,0:T(8,128)} fusion(f32[2048,512]{1,0:T(8,128)} %get-tuple-element.103, f32[2048,2048]{1,0:T(8,128)} %get-tuple-element.117, s32[]{:T(128)S(6)} %select_n.15, f32[2,512,512]{2,1,0:T(8,128)S(1)} %get-tuple-element.118, s32[]{:T(128)S(6)} %select_n.14), kind=kOutput, calls=%fused_computation.2.clone.1 | convolution fusion | flops 6443499520 | bytes 13631496 | tf_op jit(solution)/shard_map/while/body/dot_general | solution.py:21
  180.4 0.0 reduce-scatter.2.cloned.1.call-update
  180.4 35.7 %reduce-scatter.2.cloned.1.call-done = f32[256,512]{1,0:T(8,128)} async-done(((f32[2048,512]{1,0:T(8,128)}), f32[256,512]{1,0:T(8,128)}) %reduce-scatter.2.cloned.1.call-update) | async-done | bytes 524304 | tf_op jit(solution)/shard_map/reduce_scatter | solution.py:32
  216.1 1.1 multiply_reduce_fusion
  217.2 15.2 %psum.7 = f32[512]{0:T(512)S(1)} all-reduce(f32[512]{0:T(512)S(1)} %multiply_reduce_fusion), channel_id=1, replica_groups=mesh['grp'=8,'mem'=32] {'grp'}, use_global_device_ids=true, to_apply=%region_5.6 | all-reduce | flops 512 | bytes 4096 | tf_op jit(solution)/shard_map/psum | solution.py:34
  232.4 1.9 multiply_divide_fusion
  (1 shorter events, 0.0 us)
Async XLA Ops:
  6.5 148.6 %copy-start = (f32[1024,512]{1,0:T(8,128)S(1)}, f32[1024,512]{1,0:T(8,128)}, u32[]{:S(2)}) copy-start(f32[1024,512]{1,0:T(8,128)} %param.6) | copy-start | bytes 6291460
  6.5 146.2 %all-gather.2.cloned.1.call-start = ((), (), s32[]{:S(2)}) async-start(), calls=%async_computation.1 | async-start | bytes 17301504 | tf_op jit(solution)/shard_map/all_gather | solution.py:15
  7.3 208.8 %reduce-scatter.2.cloned.1.call-start = ((), (), s32[]{:S(2)}) async-start(), calls=%async_computation.2 | async-start | bytes 4718592 | tf_op jit(solution)/shard_map/reduce_scatter | solution.py:32
Sparse Core Ops, SparseCore 0:
  9.9 142.7 all-gather.1
  180.5 35.5 reduce-scatter.1
where the time goes:
time: 241 us
  waiting for transfers between devices  180 us (75%)
  matrix products  20.9 us (9%)
  blocking collectives  15.2 us (6%)
  between operations  13.4 us (6%)
  other arithmetic  4.47 us (2%)
  local copies, waits for them, and re-layouts  3.65 us (2%)
  loops' own time  3.12 us (1%)
    all_gather x1, waiting for transfers between devices, per_device(): row_piece = lax.all_gather(slab, 'mem', axis=0, tiled=True)  144 us
    reduce_scatter x1, waiting for transfers between devices, per_device(): lax.psum_scatter(partial_sums, 'grp', scatter_dimension=0, tiled=True)  35.7 us
    dot_general x2, matrix products, add_slot(): jnp.dot(columns, tile_stack[slot_index], preferred_element_type=jnp.float...  20.9 us
    psum x1, blocking collectives, per_device(): column_sums = lax.psum(jnp.sum(inflated, axis=0), 'grp')  15.2 us
  transfers between devices with their start and end apart: 2, of which 2 were waited for; matrix products, arithmetic and copies ran while one was open for 1% of the time, Pallas kernels for 0%

commit v1 on v0

--- a/solution.py
+++ b/solution.py
@@ -31,7 +31,9 @@
     window_rows = partial_sums.shape[0]
     expanded = lax.psum_scatter(partial_sums, "grp", scatter_dimension=0, tiled=True)
     inflated = expanded * expanded
-    column_sums = lax.psum(jnp.sum(inflated, axis=0), "grp")
+    block = jnp.sum(inflated, axis=0)
+    parts = lax.all_gather(block, "grp")
+    column_sums = jnp.sum(parts, axis=0)
     column_means = column_sums / window_rows
     return inflated / column_means
 

time: 241 us -> 241 us (level)
    psum x1 -> x0, blocking collectives: 15.2 us -> none  [per_device(): column_sums = lax.psum(jnp.sum(inflated, axis=0), 'grp')]
    all_gather x0 -> x1, blocking collectives: none -> 14.5 us  [per_device(): parts = lax.all_gather(block, 'grp')]
where the time goes in v1:
time: 241 us
  waiting for transfers between devices  180 us (75%)
  matrix products  20.9 us (9%)
  blocking collectives  14.5 us (6%)
  between operations  13.4 us (6%)
  other arithmetic  4.5 us (2%)
  local copies, waits for them, and re-layouts  3.65 us (2%)
  loops' own time  3.12 us (1%)
    all_gather x1, waiting for transfers between devices, per_device(): row_piece = lax.all_gather(slab, 'mem', axis=0, tiled=True)  144 us
    reduce_scatter x1, waiting for transfers between devices, per_device(): lax.psum_scatter(partial_sums, 'grp', scatter_dimension=0, tiled=True)  35.7 us
    dot_general x2, matrix products, add_slot(): jnp.dot(columns, tile_stack[slot_index], preferred_element_type=jnp.float...  20.9 us
    all_gather x1, blocking collectives, per_device(): parts = lax.all_gather(block, 'grp')  14.5 us
  transfers between devices with their start and end apart: 2, of which 2 were waited for; matrix products, arithmetic and copies ran while one was open for 1% of the time, Pallas kernels for 0%

profile of v1, /device:TPU:1, one launch (start us, length us, event | category | flops | bytes accessed | tf_op | source)
XLA Modules:
  0.0 240.5 jit_solution(8992051125408662957)
XLA Ops:
  6.5 0.0 copy-start
  6.5 0.0 all-gather.4.cloned.1.call-start
  6.5 0.7 all-gather.4.cloned.1.call-update
  7.3 0.0 reduce-scatter.2.cloned.1.call-start
  7.3 1.4 maximum_reduce_fusion
  8.8 143.9 %all-gather.4.cloned.1.call-done = f32[2048,2048]{1,0:T(8,128)} async-done(((f32[64,2048]{1,0:T(8,128)}), f32[2048,2048]{1,0:T(8,128)}) %all-gather.4.cloned.1.call-update) | async-done | bytes 16777232 | tf_op jit(solution)/shard_map/all_gather | solution.py:15
  152.7 2.5 %broadcast_in_dim.4 = f32[2048,512]{1,0:T(8,128)} broadcast(f32[]{:T(128)} %constant.7.clone.1), dimensions={} | broadcast | bytes 4194308 | tf_op jit(solution)/shard_map/broadcast_in_dim | solution.py:29
  155.2 0.0 copy-done
  155.2 25.2 %while.10 = (s32[]{:T(128)}, f32[2048,512]{1,0:T(8,128)}, s32[]{:T(128)}, s32[2]{0:T(128)S(1)}, f32[2048,2048]{1,0:T(8,128)}, /*index=5*/f32[2,512,512]{2,1,0:T(...) while((s32[]{:T(128)}, f32[2048,512]{1,0:T(8,128)}, s32[]{:T(128)}, ...), condition=%wide.region_2.3_spmd, body=%wide.region_1.2_spmd.sunk | while | flops 6443499520 | bytes 13631705 | solution.py:28
  155.8 0.6 dynamic_slice.29
  157.0 10.4 %fusion.14 = f32[2048,512]{1,0:T(8,128)} fusion(f32[2048,512]{1,0:T(8,128)} %get-tuple-element.103, f32[2048,2048]{1,0:T(8,128)} %get-tuple-element.117, s32[]{:T(128)S(6)} %select_n.15, f32[2,512,512]{2,1,0:T(8,128)S(1)} %get-tuple-element.118, s32[]{:T(128)S(6)} %select_n.14), kind=kOutput, calls=%fused_computation.2.clone.1 | convolution fusion | flops 6443499520 | bytes 13631496 | tf_op jit(solution)/shard_map/while/body/dot_general | solution.py:21
  168.1 0.6 dynamic_slice.29
  169.3 10.4 %fusion.14 = f32[2048,512]{1,0:T(8,128)} fusion(f32[2048,512]{1,0:T(8,128)} %get-tuple-element.103, f32[2048,2048]{1,0:T(8,128)} %get-tuple-element.117, s32[]{:T(128)S(6)} %select_n.15, f32[2,512,512]{2,1,0:T(8,128)S(1)} %get-tuple-element.118, s32[]{:T(128)S(6)} %select_n.14), kind=kOutput, calls=%fused_computation.2.clone.1 | convolution fusion | flops 6443499520 | bytes 13631496 | tf_op jit(solution)/shard_map/while/body/dot_general | solution.py:21
  180.4 0.0 reduce-scatter.2.cloned.1.call-update
  180.4 35.7 %reduce-scatter.2.cloned.1.call-done = f32[256,512]{1,0:T(8,128)} async-done(((f32[2048,512]{1,0:T(8,128)}), f32[256,512]{1,0:T(8,128)}) %reduce-scatter.2.cloned.1.call-update) | async-done | bytes 524304 | tf_op jit(solution)/shard_map/reduce_scatter | solution.py:32
  216.1 1.1 multiply_reduce_fusion
  217.2 14.5 %all-gather.1 = f32[8,1,512]{2,1,0:T(1,128)S(1)} all-gather(f32[1,1,512]{2,1,0:T(1,128)S(1)} %bitcast.11), channel_id=2, replica_groups=mesh['grp'=8,'mem'=32] {'grp'}, dimensions={0}, use_global_device_ids=true | all-gather | bytes 18432 | tf_op jit(solution)/shard_map/all_gather | solution.py:35
  231.8 1.9 multiply_divide_fusion
  (2 shorter events, 0.0 us)
Async XLA Ops:
  6.5 148.6 %copy-start = (f32[1024,512]{1,0:T(8,128)S(1)}, f32[1024,512]{1,0:T(8,128)}, u32[]{:S(2)}) copy-start(f32[1024,512]{1,0:T(8,128)} %param.6) | copy-start | bytes 6291460
  6.5 146.2 %all-gather.4.cloned.1.call-start = ((), (), s32[]{:S(2)}) async-start(), calls=%async_computation.1 | async-start | bytes 17301504 | tf_op jit(solution)/shard_map/all_gather | solution.py:15
  7.3 208.8 %reduce-scatter.2.cloned.1.call-start = ((), (), s32[]{:S(2)}) async-start(), calls=%async_computation.2 | async-start | bytes 4718592 | tf_op jit(solution)/shard_map/reduce_scatter | solution.py:32
Sparse Core Ops, SparseCore 0:
  9.9 142.7 all-gather.3
  180.5 35.5 reduce-scatter.1

commit v2 on v0

--- a/solution.py
+++ b/solution.py
@@ -2,6 +2,13 @@
 import jax.numpy as jnp
 from jax import lax
 from jax.sharding import PartitionSpec as P
+
+
+def exchange_gather(x, mesh_axis, dim):
+    size = lax.axis_size(mesh_axis)
+    tiles = jnp.stack([x for _ in range(size)])
+    tiles = lax.all_to_all(tiles, mesh_axis, split_axis=0, concat_axis=0)
+    return jnp.concatenate(tiles, axis=dim)
 
 
 def per_device(slab, tiles, slot_rows):
@@ -12,7 +19,7 @@
     used_slots = jnp.sum((own_rows >= 0).astype(jnp.int32))
     block_rows = jnp.maximum(own_rows, 0)
     tile_stack = tiles.reshape(slot_total, tile_size, tile_size)
-    row_piece = lax.all_gather(slab, "mem", axis=0, tiled=True)
+    row_piece = exchange_gather(slab, "mem", 0)
 
     def add_slot(slot_index, running):
         columns = lax.dynamic_slice_in_dim(

time: 241 us -> 522 us (2.17)
  waiting for transfers between devices: 180 us -> 440 us
  starting transfers between devices: 0.04 us -> 12.3 us
  local copies, waits for them, and re-layouts: 3.65 us -> 12.6 us
    all_to_all x0 -> x1, waiting for transfers between devices: none -> 369 us  [exchange_gather(): tiles = lax.all_to_all(tiles, mesh_axis, split_axis=0, concat_axis=0)]
    all_gather x1 -> x0, waiting for transfers between devices: 144 us -> none  [per_device(): row_piece = lax.all_gather(slab, 'mem', axis=0, tiled=True)]
    reduce_scatter x1, waiting for transfers between devices: 35.7 us -> 71 us  [per_device(): lax.psum_scatter(partial_sums, 'grp', scatter_dimension=0, tiled=True)]
    all_to_all x0 -> x1, starting transfers between devices: none -> 12.3 us  [exchange_gather(): tiles = lax.all_to_all(tiles, mesh_axis, split_axis=0, concat_axis=0)]
    another operation x0 -> x1, local copies, waits for them, and re-layouts: none -> 8.9 us  [exchange_gather(): tiles = jnp.stack([x for _ in range(size)])]
  transfers between devices with their start and end apart: 2 -> 2, of which waited for: 2 -> 2; matrix products, arithmetic and copies ran while one was open for 1% -> 0% of each run, Pallas kernels for 0% -> 0%
where the time goes in v2:
time: 522 us
  waiting for transfers between devices  440 us (84%)
  matrix products  20.9 us (4%)
  blocking collectives  15.2 us (3%)
  between operations  13.4 us (3%)
  local copies, waits for them, and re-layouts  12.6 us (2%)
  starting transfers between devices  12.3 us (2%)
    all_to_all x1, waiting for transfers between devices, exchange_gather(): tiles = lax.all_to_all(tiles, mesh_axis, split_axis=0, concat_axis=0)  369 us
    reduce_scatter x1, waiting for transfers between devices, per_device(): lax.psum_scatter(partial_sums, 'grp', scatter_dimension=0, tiled=True)  71 us
    dot_general x2, matrix products, add_slot(): jnp.dot(columns, tile_stack[slot_index], preferred_element_type=jnp.float...  20.9 us
    psum x1, blocking collectives, per_device(): column_sums = lax.psum(jnp.sum(inflated, axis=0), 'grp')  15.2 us
    all_to_all x1, starting transfers between devices, exchange_gather(): tiles = lax.all_to_all(tiles, mesh_axis, split_axis=0, concat_axis=0)  12.3 us
  transfers between devices with their start and end apart: 2, of which 2 were waited for; matrix products, arithmetic and copies ran while one was open for 0% of the time, Pallas kernels for 0%

profile of v2, /device:TPU:1, one launch (start us, length us, event | category | flops | bytes accessed | tf_op | source)
XLA Modules:
  0.0 522.0 jit_solution(12755862472772971109)
XLA Ops:
  6.5 8.9 %stack.2 = f32[32,64,2048]{2,1,0:T(8,128)} broadcast(f32[64,2048]{1,0:T(8,128)} %param.5), dimensions={1,2} | broadcast | bytes 17301504 | tf_op jit(solution)/shard_map/stack | solution.py:9
  15.4 0.0 copy-start.1
  15.4 12.3 %all-to-all-start = ((f32[32,64,2048]{2,1,0:T(8,128)}), f32[32,64,2048]{2,1,0:T(8,128)}, u32[]{:S(2)}, u32[]{:S(2)}) async-start(f32[32,64,2048]{2,1,0:T(8,128)} %stack.2), calls=%async_computation | async-start | bytes 33554432 | tf_op jit(solution)/shard_map/all_to_all | solution.py:10
  27.7 0.0 copy-start
  27.7 0.0 reduce-scatter.2.cloned.1.call-start
  27.8 0.0 copy-done.1
  27.8 0.8 maximum_reduce_fusion
  28.6 369.4 %all-to-all-done = f32[32,64,2048]{2,1,0:T(8,128)} async-done(((f32[32,64,2048]{2,1,0:T(8,128)}), f32[32,64,2048]{2,1,0:T(8,128)}, u32[]{:S(2)}, u32[]{:S(2)}) %all-to-all-start) | async-done | bytes 16777248 | tf_op jit(solution)/shard_map/all_to_all | solution.py:10
  398.0 2.5 broadcast_in_dim.4
  400.5 0.0 copy-done
  400.5 25.4 %while.10 = (s32[]{:T(128)}, f32[2048,512]{1,0:T(8,128)}, s32[]{:T(128)}, s32[2]{0:T(128)S(1)}, f32[2048,2048]{1,0:T(8,128)}, /*index=5*/f32[2,512,512]{2,1,0:T(...) while((s32[]{:T(128)}, f32[2048,512]{1,0:T(8,128)}, s32[]{:T(128)}, ...), condition=%wide.region_2.3_spmd, body=%wide.region_1.2_spmd.sunk | while | flops 6443499520 | bytes 13631697 | solution.py:35
  401.1 0.6 dynamic_slice.29
  402.4 10.4 %fusion.14 = f32[2048,512]{1,0:T(8,128)} fusion(f32[2048,512]{1,0:T(8,128)} %get-tuple-element.103, f32[2048,2048]{1,0:T(8,128)} %get-tuple-element.117, s32[]{:T(128)S(6)} %select_n.15, f32[2,512,512]{2,1,0:T(8,128)S(1)} %get-tuple-element.118, s32[]{:T(128)S(6)} %select_n.14), kind=kOutput, calls=%fused_computation.2.clone.1 | convolution fusion | flops 6443499520 | bytes 13631496 | tf_op jit(solution)/shard_map/while/body/dot_general | solution.py:28
  413.5 0.6 dynamic_slice.29
  414.8 10.4 %fusion.14 = f32[2048,512]{1,0:T(8,128)} fusion(f32[2048,512]{1,0:T(8,128)} %get-tuple-element.103, f32[2048,2048]{1,0:T(8,128)} %get-tuple-element.117, s32[]{:T(128)S(6)} %select_n.15, f32[2,512,512]{2,1,0:T(8,128)S(1)} %get-tuple-element.118, s32[]{:T(128)S(6)} %select_n.14), kind=kOutput, calls=%fused_computation.2.clone.1 | convolution fusion | flops 6443499520 | bytes 13631496 | tf_op jit(solution)/shard_map/while/body/dot_general | solution.py:28
  425.9 0.0 reduce-scatter.2.cloned.1.call-update
  425.9 71.0 %reduce-scatter.2.cloned.1.call-done = f32[256,512]{1,0:T(8,128)} async-done(((f32[2048,512]{1,0:T(8,128)}), f32[256,512]{1,0:T(8,128)}) %reduce-scatter.2.cloned.1.call-update) | async-done | bytes 524304 | tf_op jit(solution)/shard_map/reduce_scatter | solution.py:39
  496.9 1.1 multiply_reduce_fusion
  498.1 15.2 %psum.7 = f32[512]{0:T(512)S(1)} all-reduce(f32[512]{0:T(512)S(1)} %multiply_reduce_fusion), channel_id=1, replica_groups=mesh['grp'=8,'mem'=32] {'grp'}, use_global_device_ids=true, to_apply=%region_5.6 | all-reduce | flops 512 | bytes 4096 | tf_op jit(solution)/shard_map/psum | solution.py:41
  513.2 1.9 multiply_divide_fusion
  (1 shorter events, 0.0 us)
Async XLA Ops:
  15.4 12.4 %copy-start.1 = (s32[2,32]{1,0:T(2,128)S(1)}, s32[2,32]{1,0:T(2,128)}, u32[]{:S(2)}) copy-start(s32[2,32]{1,0:T(2,128)} %param.7) | copy-start | bytes 772
  15.4 382.6 %all-to-all-start = ((f32[32,64,2048]{2,1,0:T(8,128)}), f32[32,64,2048]{2,1,0:T(8,128)}, u32[]{:S(2)}, u32[]{:S(2)}) async-start(f32[32,64,2048]{2,1,0:T(8,128)} %stack.2), calls=%async_computation | async-start | bytes 33554432 | tf_op jit(solution)/shard_map/all_to_all | solution.py:10
  27.7 372.7 %copy-start = (f32[1024,512]{1,0:T(8,128)S(1)}, f32[1024,512]{1,0:T(8,128)}, u32[]{:S(2)}) copy-start(f32[1024,512]{1,0:T(8,128)} %param.6) | copy-start | bytes 6291460
  27.7 469.2 %reduce-scatter.2.cloned.1.call-start = ((), (), s32[]{:S(2)}) async-start(), calls=%async_computation.2 | async-start | bytes 4718592 | tf_op jit(solution)/shard_map/reduce_scatter | solution.py:39
Sparse Core Ops, SparseCore 0:
  426.0 70.8 reduce-scatter.1
